TPU v7x, 512 devices: a whole 4x4x16 slice. The times are simulated.
512 devices in a mesh: orb: 64 (over z, y), fft: 8 (over x, core).
Axes of the slice: x: 4, y: 4, z: 16, core: 2. Of those that a mesh axis runs over, the one named last changes fastest.
Arguments:
- orbitals: bfloat16 [512, 256, 256], P('orb', 'fft'), may hold values from -6 to 6
- kernel: float32 [256, 256], P('fft'), may hold values from 0.02 to 2
- partner_owner: int32 [512, 2, 1], P('orb'), may hold values from 0 to 63; in each aligned block of 16 rows (0 to 15, 16 to 31, ..., all dimensions but the last counted through in order) at most 2 rows name the same one
- partner_local: int32 [512, 2], P('orb'), may hold values from 0 to 7
Outputs:
- exchange_term: float32 [512, 256, 256], P('orb', 'fft')
Inputs may be any that keep to these rules, and one draw needn't show every extreme that they name: `partner_owner`: among the 16 partners named on one index of orb, no owner is named more than 2 times, a bound that some block reaches; every owner is named somewhere.
All inputs are finite; a program needn't handle non-finite values.
Results may differ from a plain program's by a relative error of at most 0.0004.
Values may be sent and summed in bfloat16 or wider, within the bound.
No kernel may reach another device: no remote copies, remote signals or barrier semaphores. Data moves between devices by JAX's collectives and lax.ppermute only.
A program may use at most 64 MiB of HBM per device.

v0:
```python
import math
import jax
import jax.numpy as jnp
from jax import lax
from jax.sharding import PartitionSpec as P


def sent_to_all(x, axis):
    count = lax.axis_size(axis)
    return lax.all_to_all(jnp.broadcast_to(x[None], (count, *x.shape)), axis, 0, 0, tiled=True)


def in_order(tiles, dim):
    tiles = jnp.moveaxis(tiles, 0, dim)
    shape = tiles.shape
    return tiles.reshape(*shape[:dim], shape[dim] * shape[dim + 1], *shape[dim + 2 :])


def gathered_copies(x, axis, dim):
    tiles = sent_to_all(x, axis)
    return in_order(tiles, dim)


def tables(length):
    series = jnp.arange(length, dtype=jnp.int32)
    phase = series[:, None] * series[None, :] % length
    angle = phase.astype(jnp.float32) * (2.0 * math.pi / length)
    return (jnp.cos(angle), jnp.sin(angle))


def product(form, left, right):
    return jnp.einsum(form, left, right, precision=lax.Precision.HIGHEST)


def group_potential(density, kernel):
    grouped = lax.all_to_all(density, "fft", split_axis=0, concat_axis=1, tiled=True)
    whole = gathered_copies(kernel, "fft", 0)
    full_x = grouped.shape[1]
    width_y = grouped.shape[2]
    cos_y, sin_y = tables(width_y)
    cos_x, sin_x = tables(full_x)
    real_y = product("txy,yk->txk", grouped, cos_y)
    imag_y = -product("txy,yk->txk", grouped, sin_y)
    f_real = product("txk,xq->tqk", real_y, cos_x) + product("txk,xq->tqk", imag_y, sin_x)
    f_imag = product("txk,xq->tqk", imag_y, cos_x) - product("txk,xq->tqk", real_y, sin_x)
    weight = whole.T
    g_real = weight[None] * f_real
    g_imag = weight[None] * f_imag
    h_real = product("tqk,qx->txk", g_real, cos_x) - product("tqk,qx->txk", g_imag, sin_x)
    h_imag = product("tqk,qx->txk", g_real, sin_x) + product("tqk,qx->txk", g_imag, cos_x)
    spread = product("txk,ky->txy", h_real, cos_y) - product("txk,ky->txy", h_imag, sin_y)
    spread = spread / (full_x * width_y)
    return lax.all_to_all(spread, "fft", split_axis=1, concat_axis=0, tiled=True)


def on_device(orbitals, kernel, partner_owner, partner_local):
    peer_count = lax.axis_size("orb")
    orb_dev, rows_x, width_y = orbitals.shape
    task_count = partner_local.shape[0]
    wanted_count = 2 * task_count
    capacity = max(2, (4 * task_count + peer_count - 1) // peer_count)
    owner_ids = partner_owner.reshape(wanted_count)
    local_ids = partner_local.reshape(wanted_count)
    peer_ids = jnp.arange(peer_count, dtype=jnp.int32)
    owner_hot = (owner_ids[:, None] == peer_ids[None, :]).astype(jnp.int32)
    earlier = jnp.cumsum(owner_hot, axis=0) - owner_hot
    position = jnp.sum(earlier * owner_hot, axis=1)
    target = owner_ids * capacity + position
    slot_ids = jnp.arange(peer_count * capacity, dtype=jnp.int32)
    placed = target[:, None] == slot_ids[None, :]
    wanted = jnp.max(jnp.where(placed, local_ids[:, None], -1), axis=0).reshape(
        peer_count, capacity
    )
    asked = lax.all_to_all(wanted, "orb", split_axis=0, concat_axis=0, tiled=True)
    flat_asked = asked.reshape(peer_count * capacity)
    present = flat_asked >= 0
    picked = jnp.take(orbitals, jnp.clip(flat_asked, 0, orb_dev - 1), axis=0)
    served = jnp.where(present[:, None, None], picked, jnp.zeros_like(picked))
    served = served.reshape(peer_count, capacity, rows_x, width_y)
    arrived = lax.all_to_all(served, "orb", split_axis=0, concat_axis=0, tiled=True)
    arrived = arrived.reshape(peer_count * capacity, rows_x, width_y)
    chosen = (
        jnp.take(arrived, target, axis=0)
        .reshape(task_count, 2, rows_x, width_y)
        .astype(jnp.float32)
    )
    left_orbital = chosen[:, 0]
    right_orbital = chosen[:, 1]
    density = left_orbital * right_orbital
    potential = group_potential(density, kernel)
    contrib = jnp.stack([potential * right_orbital, potential * left_orbital], axis=1)
    contrib = contrib.reshape(wanted_count, rows_x, width_y)
    outgoing = (
        jnp.zeros((peer_count * capacity, rows_x, width_y), jnp.float32).at[target].set(contrib)
    )
    outgoing = outgoing.reshape(peer_count, capacity, rows_x, width_y)
    incoming = lax.all_to_all(outgoing, "orb", split_axis=0, concat_axis=0, tiled=True)
    incoming = incoming.reshape(peer_count * capacity, rows_x * width_y)
    select = (flat_asked[None, :] == jnp.arange(orb_dev, dtype=jnp.int32)[:, None]).astype(
        jnp.float32
    )
    total = jnp.dot(select, incoming, precision=lax.Precision.HIGHEST)
    return (-total).reshape(orb_dev, rows_x, width_y)


def solution(mesh):
    in_specs = (P("orb", "fft", None), P("fft", None), P("orb", None, None), P("orb", None))
    out_specs = P("orb", "fft", None)
    return jax.shard_map(
        on_device, mesh=mesh, in_specs=in_specs, out_specs=out_specs, check_vma=False
    )
```

profile of v0, /device:TPU:8, one launch (start us, length us, event | category | flops | bytes accessed | tf_op | source)
XLA Modules:
  0.0 404.2 jit_solution(12548411028635859213)
XLA Ops:
  2.3 32.3 %all_to_all.45 = s32[64,1,2]{2,1,0:T(1,128)S(1)} all-to-all(s32[64,1,2]{2,1,0:T(1,128)S(1)} %bitcast.64), channel_id=1, replica_groups=mesh['orb'=64,'fft'=8] {'orb'}, dimensions={0} | all-to-all | bytes 1024 | tf_op jit(solution)/shard_map/all_to_all | solution.py:74
  35.9 1.6 select_select_fusion
  37.5 5.5 %all-to-all-start.2 = ((bf16[64,2,32,256]{3,2,1,0:T(8,128)(2,1)}), bf16[64,2,32,256]{3,2,1,0:T(8,128)(2,1)S(1)}, u32[]{:S(2)}, u32[]{:S(2)}) async-start(bf16[64,2,32,256]{3,2,1,0:T(8,128)(2,1)} %select_select_fusion), calls=%async_computation.2 | async-start | bytes 4194304 | tf_op jit(solution)/shard_map/all_to_all | solution.py:80
  43.5 98.6 %all-to-all-done.2 = bf16[64,2,32,256]{3,2,1,0:T(8,128)(2,1)S(1)} async-done(((bf16[64,2,32,256]{3,2,1,0:T(8,128)(2,1)}), bf16[64,2,32,256]{3,2,1,0:T(8,128)(2,1)S(1)}, u32[]{:S(2)}, u32[]{:S(2)}) %all-to-all-start.2) | async-done | bytes 2097184 | tf_op jit(solution)/shard_map/all_to_all | solution.py:80
  142.8 4.3 %all-to-all-start.1 = ((f32[8,32,256]{2,1,0:T(8,128)}), f32[8,32,256]{2,1,0:T(8,128)S(1)}, u32[]{:S(2)}, u32[]{:S(2)}) async-start(f32[8,32,256]{2,1,0:T(8,128)} %broadcast_in_dim.70), calls=%async_computation.1 | async-start | bytes 524288 | tf_op jit(solution)/shard_map/all_to_all | solution.py:10
  148.6 6.1 %all-to-all-done.1 = f32[8,32,256]{2,1,0:T(8,128)S(1)} async-done(((f32[8,32,256]{2,1,0:T(8,128)}), f32[8,32,256]{2,1,0:T(8,128)S(1)}, u32[]{:S(2)}, u32[]{:S(2)}) %all-to-all-start.1) | async-done | bytes 262176 | tf_op jit(solution)/shard_map/all_to_all | solution.py:10
  154.6 3.6 all-to-all-start.3
  158.4 7.1 %all-to-all-done.3 = f32[8,32,256]{2,1,0:T(8,128)S(1)} async-done(((f32[8,32,256]{2,1,0:T(8,128)}), f32[8,32,256]{2,1,0:T(8,128)S(1)}, u32[]{:S(2)}, u32[]{:S(2)}) %all-to-all-start.3) | async-done | bytes 262176 | tf_op jit(solution)/shard_map/all_to_all | solution.py:36
  168.2 1.8 fusion.19
  170.0 1.8 fusion.15
  171.8 1.8 fusion.3
  173.5 1.8 fusion.24
  175.3 1.8 fusion.17
  177.1 1.8 fusion.2
  178.9 1.8 convolution_subtract_fusion.1
  180.6 2.0 convolution_add_fusion
  184.0 1.4 fusion.1
  185.6 9.9 %all_to_all.46 = f32[1,256,256]{2,0,1:T(1,128)S(1)} all-to-all(f32[1,256,256]{2,0,1:T(1,128)S(1)} %copy.66), channel_id=1, replica_groups=mesh['orb'=64,'fft'=8] {'fft'}, dimensions={1} | all-to-all | bytes 524288 | tf_op jit(solution)/shard_map/all_to_all | solution.py:53
  195.7 2.5 broadcast_in_dim.69
  198.2 2.6 scatter_fusion
  200.8 6.1 %all-to-all-start.5 = ((f32[64,2,32,256]{3,2,1,0:T(8,128)}), f32[64,2,32,256]{3,2,1,0:T(8,128)}, u32[]{:S(2)}, u32[]{:S(2)}) async-start(f32[64,2,32,256]{3,2,1,0:T(8,128)} %bitcast.53), calls=%async_computation.5 | async-start | bytes 8388608 | tf_op jit(solution)/shard_map/all_to_all | solution.py:97
  208.3 188.2 %all-to-all-done.5 = f32[64,2,32,256]{3,2,1,0:T(8,128)} async-done(((f32[64,2,32,256]{3,2,1,0:T(8,128)}), f32[64,2,32,256]{3,2,1,0:T(8,128)}, u32[]{:S(2)}, u32[]{:S(2)}) %all-to-all-start.5) | async-done | bytes 4194336 | tf_op jit(solution)/shard_map/all_to_all | solution.py:97
  396.4 5.5 %copy.69 = f32[16,8,32,256]{3,1,2,0:T(8,128)S(1)} copy(f32[16,8,32,256]{3,2,1,0:T(8,128)} %bitcast.23) | data formatting | bytes 8388608
  401.9 1.5 convolution_negate_fusion
  (52 shorter events, 12.8 us)
Async XLA Ops:
  0.0 35.2 %copy-start = (bf16[8,32,256]{2,1,0:T(8,128)(2,1)S(1)}, bf16[8,32,256]{2,1,0:T(8,128)(2,1)}, u32[]{:S(2)}) copy-start(bf16[8,32,256]{2,1,0:T(8,128)(2,1)} %param.4) | copy-start | bytes 393220
  37.5 5.6 %copy-start.2 = (s32[8,2,1]{0,2,1:T(1,128)S(1)}, s32[8,2,1]{0,2,1:T(1,128)}, u32[]{:S(2)}) copy-start(s32[8,2,1]{0,2,1:T(1,128)} %param.6) | copy-start | bytes 196
  37.5 104.6 %copy-start.1 = (f32[32,256]{1,0:T(8,128)S(1)}, f32[32,256]{1,0:T(8,128)}, u32[]{:S(2)}) copy-start(f32[32,256]{1,0:T(8,128)} %param.5) | copy-start | bytes 98308
  37.5 104.6 %all-to-all-start.2 = ((bf16[64,2,32,256]{3,2,1,0:T(8,128)(2,1)}), bf16[64,2,32,256]{3,2,1,0:T(8,128)(2,1)S(1)}, u32[]{:S(2)}, u32[]{:S(2)}) async-start(bf16[64,2,32,256]{3,2,1,0:T(8,128)(2,1)} %select_select_fusion), calls=%async_computation.2 | async-start | bytes 4194304 | tf_op jit(solution)/shard_map/all_to_all | solution.py:80
  142.8 11.8 %all-to-all-start.1 = ((f32[8,32,256]{2,1,0:T(8,128)}), f32[8,32,256]{2,1,0:T(8,128)S(1)}, u32[]{:S(2)}, u32[]{:S(2)}) async-start(f32[8,32,256]{2,1,0:T(8,128)} %broadcast_in_dim.70), calls=%async_computation.1 | async-start | bytes 524288 | tf_op jit(solution)/shard_map/all_to_all | solution.py:10
  154.6 10.9 %all-to-all-start.3 = ((f32[8,32,256]{2,1,0:T(8,128)}), f32[8,32,256]{2,1,0:T(8,128)S(1)}, u32[]{:S(2)}, u32[]{:S(2)}) async-start(f32[8,32,256]{2,1,0:T(8,128)} %multiply_bitcast_fusion), calls=%async_computation.3 | async-start | bytes 524288 | tf_op jit(solution)/shard_map/all_to_all | solution.py:36
  200.8 195.7 %all-to-all-start.5 = ((f32[64,2,32,256]{3,2,1,0:T(8,128)}), f32[64,2,32,256]{3,2,1,0:T(8,128)}, u32[]{:S(2)}, u32[]{:S(2)}) async-start(f32[64,2,32,256]{3,2,1,0:T(8,128)} %bitcast.53), calls=%async_computation.5 | async-start | bytes 8388608 | tf_op jit(solution)/shard_map/all_to_all | solution.py:97
where the time goes:
time: 405 us; the launch traced here: 404 us
  waiting for transfers between devices  300 us (74%)
  blocking collectives  42.3 us (10%)
  matrix products  21.3 us (5%)
  starting transfers between devices  19.5 us (5%)
  local copies, waits for them, and re-layouts  17.2 us (4%)
    all_to_all x1, waiting for transfers between devices, on_device(): lax.all_to_all(outgoing, 'orb', split_axis=0, concat_axis=0, tiled=True)  188 us
    all_to_all x1, waiting for transfers between devices, on_device(): lax.all_to_all(served, 'orb', split_axis=0, concat_axis=0, tiled=True)  98.6 us
    all_to_all x1, blocking collectives, on_device(): lax.all_to_all(wanted, 'orb', split_axis=0, concat_axis=0, tiled=True)  32.3 us
    dot_general x12, matrix products, product(): return jnp.einsum(form, left, right, precision=lax.Precision.HIGHEST)  19.8 us
    all_to_all x1, blocking collectives, group_potential(): lax.all_to_all(spread, 'fft', split_axis=1, concat_axis=0, tiled=True)  9.91 us
  transfers between devices with their start and end apart: 4, of which 4 were waited for; matrix products, arithmetic and copies ran while one was open for 1% of the time, Pallas kernels for 0%

commit v1 on v0

--- a/solution.py
+++ b/solution.py
@@ -33,7 +33,10 @@
 
 
 def group_potential(density, kernel):
-    grouped = lax.all_to_all(density, "fft", split_axis=0, concat_axis=1, tiled=True)
+    grouped = jnp.concatenate(
+        lax.all_to_all(jnp.stack(jnp.split(density, lax.axis_size("fft"), axis=0)), "fft", 0, 0),
+        axis=1,
+    )
     whole = gathered_copies(kernel, "fft", 0)
     full_x = grouped.shape[1]
     width_y = grouped.shape[2]

time: 405 us -> 405 us (level)
  no operation moved by 1% of the time
where the time goes in v1:
time: 405 us; the launch traced here: 404 us
  waiting for transfers between devices  300 us (74%)
  blocking collectives  42.3 us (10%)
  matrix products  21.3 us (5%)
  starting transfers between devices  19.5 us (5%)
  local copies, waits for them, and re-layouts  17.2 us (4%)
    all_to_all x1, waiting for transfers between devices, on_device(): lax.all_to_all(outgoing, 'orb', split_axis=0, concat_axis=0, tiled=True)  188 us
    all_to_all x1, waiting for transfers between devices, on_device(): lax.all_to_all(served, 'orb', split_axis=0, concat_axis=0, tiled=True)  98.6 us
    all_to_all x1, blocking collectives, on_device(): lax.all_to_all(wanted, 'orb', split_axis=0, concat_axis=0, tiled=True)  32.3 us
    dot_general x12, matrix products, product(): return jnp.einsum(form, left, right, precision=lax.Precision.HIGHEST)  19.8 us
    all_to_all x1, blocking collectives, group_potential(): lax.all_to_all(spread, 'fft', split_axis=1, concat_axis=0, tiled=True)  9.91 us
  transfers between devices with their start and end apart: 4, of which 4 were waited for; matrix products, arithmetic and copies ran while one was open for 1% of the time, Pallas kernels for 0%

profile of v1, /device:TPU:8, one launch (start us, length us, event | category | flops | bytes accessed | tf_op | source)
XLA Modules:
  0.0 404.2 jit_solution(12548411028635859213)
XLA Ops:
  2.3 32.3 %all_to_all.41 = s32[64,1,2]{2,1,0:T(1,128)S(1)} all-to-all(s32[64,1,2]{2,1,0:T(1,128)S(1)} %bitcast.62), channel_id=1, replica_groups=mesh['orb'=64,'fft'=8] {'orb'}, dimensions={0} | all-to-all | bytes 1024 | tf_op jit(solution)/shard_map/all_to_all | solution.py:77
  35.9 1.6 select_select_fusion
  37.5 5.5 %all-to-all-start.2 = ((bf16[64,2,32,256]{3,2,1,0:T(8,128)(2,1)}), bf16[64,2,32,256]{3,2,1,0:T(8,128)(2,1)S(1)}, u32[]{:S(2)}, u32[]{:S(2)}) async-start(bf16[64,2,32,256]{3,2,1,0:T(8,128)(2,1)} %select_select_fusion), calls=%async_computation.2 | async-start | bytes 4194304 | tf_op jit(solution)/shard_map/all_to_all | solution.py:83
  43.5 98.6 %all-to-all-done.2 = bf16[64,2,32,256]{3,2,1,0:T(8,128)(2,1)S(1)} async-done(((bf16[64,2,32,256]{3,2,1,0:T(8,128)(2,1)}), bf16[64,2,32,256]{3,2,1,0:T(8,128)(2,1)S(1)}, u32[]{:S(2)}, u32[]{:S(2)}) %all-to-all-start.2) | async-done | bytes 2097184 | tf_op jit(solution)/shard_map/all_to_all | solution.py:83
  142.8 4.3 %all-to-all-start.1 = ((f32[8,32,256]{2,1,0:T(8,128)}), f32[8,32,256]{2,1,0:T(8,128)S(1)}, u32[]{:S(2)}, u32[]{:S(2)}) async-start(f32[8,32,256]{2,1,0:T(8,128)} %broadcast_in_dim.70), calls=%async_computation.1 | async-start | bytes 524288 | tf_op jit(solution)/shard_map/all_to_all | solution.py:10
  148.6 6.1 %all-to-all-done.1 = f32[8,32,256]{2,1,0:T(8,128)S(1)} async-done(((f32[8,32,256]{2,1,0:T(8,128)}), f32[8,32,256]{2,1,0:T(8,128)S(1)}, u32[]{:S(2)}, u32[]{:S(2)}) %all-to-all-start.1) | async-done | bytes 262176 | tf_op jit(solution)/shard_map/all_to_all | solution.py:10
  154.6 3.6 all-to-all-start.3
  158.4 7.1 %all-to-all-done.3 = f32[8,1,32,256]{3,2,1,0:T(8,128)S(1)} async-done(((f32[8,1,32,256]{3,2,1,0:T(8,128)}), f32[8,1,32,256]{3,2,1,0:T(8,128)S(1)}, u32[]{:S(2)}, u32[]{:S(2)}) %all-to-all-start.3) | async-done | bytes 262176 | tf_op jit(solution)/shard_map/all_to_all | solution.py:37
  168.2 1.8 fusion.19
  170.0 1.8 fusion.15
  171.8 1.8 fusion.3
  173.5 1.8 fusion.24
  175.3 1.8 fusion.17
  177.1 1.8 fusion.2
  178.9 1.8 convolution_subtract_fusion.1
  180.6 2.0 convolution_add_fusion
  184.0 1.4 fusion.1
  185.6 9.9 %all_to_all.42 = f32[1,256,256]{2,0,1:T(1,128)S(1)} all-to-all(f32[1,256,256]{2,0,1:T(1,128)S(1)} %copy.66), channel_id=1, replica_groups=mesh['orb'=64,'fft'=8] {'fft'}, dimensions={1} | all-to-all | bytes 524288 | tf_op jit(solution)/shard_map/all_to_all | solution.py:56
  195.7 2.5 broadcast_in_dim.69
  198.2 2.6 scatter_fusion
  200.8 6.1 %all-to-all-start.5 = ((f32[64,2,32,256]{3,2,1,0:T(8,128)}), f32[64,2,32,256]{3,2,1,0:T(8,128)}, u32[]{:S(2)}, u32[]{:S(2)}) async-start(f32[64,2,32,256]{3,2,1,0:T(8,128)} %bitcast.51), calls=%async_computation.5 | async-start | bytes 8388608 | tf_op jit(solution)/shard_map/all_to_all | solution.py:100
  208.3 188.2 %all-to-all-done.5 = f32[64,2,32,256]{3,2,1,0:T(8,128)} async-done(((f32[64,2,32,256]{3,2,1,0:T(8,128)}), f32[64,2,32,256]{3,2,1,0:T(8,128)}, u32[]{:S(2)}, u32[]{:S(2)}) %all-to-all-start.5) | async-done | bytes 4194336 | tf_op jit(solution)/shard_map/all_to_all | solution.py:100
  396.4 5.5 %copy.69 = f32[16,8,32,256]{3,1,2,0:T(8,128)S(1)} copy(f32[16,8,32,256]{3,2,1,0:T(8,128)} %bitcast.22) | data formatting | bytes 8388608
  401.9 1.5 convolution_negate_fusion
  (52 shorter events, 12.8 us)
Async XLA Ops:
  0.0 35.2 %copy-start = (bf16[8,32,256]{2,1,0:T(8,128)(2,1)S(1)}, bf16[8,32,256]{2,1,0:T(8,128)(2,1)}, u32[]{:S(2)}) copy-start(bf16[8,32,256]{2,1,0:T(8,128)(2,1)} %param.4) | copy-start | bytes 393220
  37.5 5.6 %copy-start.2 = (s32[8,2,1]{0,2,1:T(1,128)S(1)}, s32[8,2,1]{0,2,1:T(1,128)}, u32[]{:S(2)}) copy-start(s32[8,2,1]{0,2,1:T(1,128)} %param.6) | copy-start | bytes 196
  37.5 104.6 %copy-start.1 = (f32[32,256]{1,0:T(8,128)S(1)}, f32[32,256]{1,0:T(8,128)}, u32[]{:S(2)}) copy-start(f32[32,256]{1,0:T(8,128)} %param.5) | copy-start | bytes 98308
  37.5 104.6 %all-to-all-start.2 = ((bf16[64,2,32,256]{3,2,1,0:T(8,128)(2,1)}), bf16[64,2,32,256]{3,2,1,0:T(8,128)(2,1)S(1)}, u32[]{:S(2)}, u32[]{:S(2)}) async-start(bf16[64,2,32,256]{3,2,1,0:T(8,128)(2,1)} %select_select_fusion), calls=%async_computation.2 | async-start | bytes 4194304 | tf_op jit(solution)/shard_map/all_to_all | solution.py:83
  142.8 11.8 %all-to-all-start.1 = ((f32[8,32,256]{2,1,0:T(8,128)}), f32[8,32,256]{2,1,0:T(8,128)S(1)}, u32[]{:S(2)}, u32[]{:S(2)}) async-start(f32[8,32,256]{2,1,0:T(8,128)} %broadcast_in_dim.70), calls=%async_computation.1 | async-start | bytes 524288 | tf_op jit(solution)/shard_map/all_to_all | solution.py:10
  154.6 10.9 %all-to-all-start.3 = ((f32[8,1,32,256]{3,2,1,0:T(8,128)}), f32[8,1,32,256]{3,2,1,0:T(8,128)S(1)}, u32[]{:S(2)}, u32[]{:S(2)}) async-start(f32[8,1,32,256]{3,2,1,0:T(8,128)} %slice_multiply_fusion.1), calls=%async_computation.3 | async-start | bytes 524288 | tf_op jit(solution)/shard_map/all_to_all | solution.py:37
  200.8 195.7 %all-to-all-start.5 = ((f32[64,2,32,256]{3,2,1,0:T(8,128)}), f32[64,2,32,256]{3,2,1,0:T(8,128)}, u32[]{:S(2)}, u32[]{:S(2)}) async-start(f32[64,2,32,256]{3,2,1,0:T(8,128)} %bitcast.51), calls=%async_computation.5 | async-start | bytes 8388608 | tf_op jit(solution)/shard_map/all_to_all | solution.py:100
